TPU v7x, 32 devices: a whole 2x2x4 slice. The times are simulated.
32 devices in a mesh: gx: 4 (over y, core), gy: 4 (over z), gz: 2 (over x).
Axes of the slice: x: 2, y: 2, z: 4, core: 2. Of those that a mesh axis runs over, the one named last changes fastest.
Arguments:
- inputs: bfloat16 [32768, 2048], P(('gx', 'gy', 'gz')), may hold values from -6 to 6
- cotangent: bfloat16 [32768, 4096], P(('gx', 'gy', 'gz')), may hold values from -0.032958984 to 0.032958984
- master: float32 [2048, 4096], P(('gx', 'gy', 'gz')), may hold values from -3 to 3
- accum: float32 [2048, 4096], P(('gx', 'gy', 'gz')), may hold values from 0.05 to 1
Outputs:
- new_master: float32 [2048, 4096], P(('gx', 'gy', 'gz'))
- new_accum: float32 [2048, 4096], P(('gx', 'gy', 'gz'))
All inputs are finite; a program needn't handle non-finite values.
Results may differ from a plain program's by a relative error of at most 0.0003.
Values sent between devices are 32-bit elements; how exact they have to be, the bound alone decides.
A program may use at most 128 MiB of HBM per device.

v0:
```python
import jax
import jax.numpy as jnp
from jax import lax
from jax.sharding import PartitionSpec as P

D = 4096
ROWS = 2048


def shards(inputs, cotangent, master, accum):
    partial_value = lax.psum_scatter(
        lax.dot_general(
            inputs, cotangent, (((0,), (0,)), ((), ())), preferred_element_type=jnp.float32
        ),
        ("gx", "gy"),
        scatter_dimension=0,
        tiled=True,
    )
    gradient = lax.psum_scatter(partial_value, "gz", scatter_dimension=0, tiled=True)
    squares = lax.psum(jnp.sum(gradient * gradient), ("gx", "gy", "gz"))
    limit = 0.5 * jnp.sqrt(jnp.float32(ROWS * D))
    factor = limit / jnp.maximum(jnp.sqrt(squares), limit)
    scaled = factor * gradient
    new_accum = accum + scaled * scaled
    new_master = master - 0.5 * scaled / jnp.sqrt(new_accum)
    return (new_master, new_accum)


def solution(mesh):
    return jax.shard_map(
        shards,
        mesh=mesh,
        in_specs=(
            P(("gx", "gy", "gz"), None),
            P(("gx", "gy", "gz"), None),
            P(("gx", "gy", "gz"), None),
            P(("gx", "gy", "gz"), None),
        ),
        out_specs=(P(("gx", "gy", "gz"), None), P(("gx", "gy", "gz"), None)),
        check_vma=False,
    )
```

profile of v0, /device:TPU:0, one launch (start us, length us, event | category | flops | bytes accessed | tf_op | source)
XLA Modules:
  0.0 451.2 jit_solution(13843896567224608363)
XLA Ops:
  7.2 0.0 reduce-scatter.3.cloned.1.call-start
  7.2 25.3 %fusion = f32[2048,4096]{1,0:T(8,128)} fusion(bf16[1024,2048]{1,0:T(8,128)(2,1)} %param.4, bf16[1024,4096]{1,0:T(8,128)(2,1)} %param.5), kind=kOutput, calls=%fused_computation.3 | convolution fusion | flops 17179869184 | bytes 46137344 | tf_op jit(solution)/shard_map/dot_general | solution.py:12
  32.5 0.0 copy-start
  32.5 0.0 copy-start.1
  32.5 0.0 reduce-scatter.3.cloned.1.call-update
  32.6 0.0 reduce-scatter.5.cloned.1.call-start
  32.6 333.3 %reduce-scatter.3.cloned.1.call-done = f32[128,4096]{1,0:T(8,128)} async-done(((f32[2048,4096]{1,0:T(8,128)}), f32[128,4096]{1,0:T(8,128)}) %reduce-scatter.3.cloned.1.call-update) | async-done | bytes 2097168 | tf_op jit(solution)/shard_map/reduce_scatter | solution.py:11
  365.9 0.0 reduce-scatter.5.cloned.1.call-update
  366.0 33.3 %reduce-scatter.5.cloned.1.call-done = f32[64,4096]{1,0:T(8,128)} async-done(((f32[128,4096]{1,0:T(8,128)}), f32[64,4096]{1,0:T(8,128)}) %reduce-scatter.5.cloned.1.call-update) | async-done | bytes 1048592 | tf_op jit(solution)/shard_map/reduce_scatter | solution.py:19
  399.2 2.1 multiply_reduce_fusion
  401.3 39.5 %psum.7 = f32[]{:T(128)} all-reduce(f32[]{:T(128)} %multiply_reduce_fusion), channel_id=1, replica_groups=mesh['gx'=4,'gy'=4,'gz'=2] {'gx','gy','gz'}, use_global_device_ids=true, to_apply=%region_3.0 | all-reduce | flops 1 | bytes 8 | tf_op jit(solution)/shard_map/psum | solution.py:20
  441.5 0.0 copy-done
  441.5 0.0 copy-done.1
  441.5 2.8 multiply_subtract_fusion
Async XLA Ops:
  7.2 358.8 %reduce-scatter.3.cloned.1.call-start = ((), (), s32[]{:S(2)}) async-start(), calls=%async_computation.2 | async-start | bytes 35651584 | tf_op jit(solution)/shard_map/reduce_scatter | solution.py:11
  32.5 409.0 %copy-start = (f32[64,4096]{1,0:T(8,128)S(1)}, f32[64,4096]{1,0:T(8,128)}, u32[]{:S(2)}) copy-start(f32[64,4096]{1,0:T(8,128)} %param.6) | copy-start | bytes 3145732
  32.5 409.0 %copy-start.1 = (f32[64,4096]{1,0:T(8,128)S(1)}, f32[64,4096]{1,0:T(8,128)}, u32[]{:S(2)}) copy-start(f32[64,4096]{1,0:T(8,128)} %param.7) | copy-start | bytes 3145732
  32.6 366.7 %reduce-scatter.5.cloned.1.call-start = ((), (), s32[]{:S(2)}) async-start(), calls=%async_computation.3 | async-start | bytes 3145728 | tf_op jit(solution)/shard_map/reduce_scatter | solution.py:19
Sparse Core Ops, SparseCore 0:
  32.7 333.2 reduce-scatter.2
  368.2 30.9 reduce-scatter.4
where the time goes:
time: 451 us
  waiting for transfers between devices  367 us (81%)
  blocking collectives  39.5 us (9%)
  matrix products  25.3 us (6%)
  between operations  14.8 us (3%)
  other arithmetic  4.88 us (1%)
    reduce_scatter x1, waiting for transfers between devices, shards(): lax.psum_scatter(lax.dot_general(inputs, cotangent, (((0,), (0,)), ((), (...  333 us
    psum x1, blocking collectives, shards(): squares = lax.psum(jnp.sum(gradient * gradient), ('gx', 'gy', 'gz'))  39.5 us
    reduce_scatter x1, waiting for transfers between devices, shards(): lax.psum_scatter(partial_value, 'gz', scatter_dimension=0, tiled=True)  33.3 us
    dot_general x1, matrix products, shards(): lax.dot_general(inputs, cotangent, (((0,), (0,)), ((), ())), preferred_el...  25.3 us
  transfers between devices with their start and end apart: 2, of which 2 were waited for; matrix products, arithmetic and copies ran while one was open for 0% of the time, Pallas kernels for 0%

commit v1 on v0

v1 whole, which is shorter than its diff:
```python
import functools
import math

import jax
import jax.numpy as jnp
from jax import lax
from jax.experimental import pallas as pl
from jax.experimental.pallas import tpu as pltpu
from jax.sharding import PartitionSpec as P

AXES = ("gx", "gy", "gz")
MESH = pl.DeviceIdType.MESH
PATTERN = "XYZXYUXYXYZXYUXY"


def bits_of(n):
    return n.bit_length() - 1


def plan(sizes):
    bits = [(a, 1 << b) for a, n in zip(AXES, sizes) for b in reversed(range(bits_of(n)))]
    core = bits.index(("gx", 1))
    ys = [i for i, (a, w) in enumerate(bits) if a == "gx" and w > 1]
    zs = [i for i, (a, w) in enumerate(bits) if a == "gy"][::-1]
    xs = [i for i, (a, w) in enumerate(bits) if a == "gz"][::-1]
    orders = {
        "X": xs + ys + zs,
        "Y": ys + xs + zs,
        "Z": zs[:1] + xs + ys + zs[1:],
        "U": zs[:1] + ys + xs + zs[1:],
    }
    return bits, core, orders


def events(bits, orders, pieces):
    free, ready, out = {}, [], []
    for k in range(len(pieces)):
        ready.append((k + 1.0, 0, k))
    while ready:
        ready.sort()
        at, phase, k = ready.pop(0)
        out.append((phase, k))
        order = orders[pieces[k]]
        if phase < len(order):
            link = bits[order[phase]]
            cost = 6.0 / (1 << phase) * (2 if link[1] > 1 and link[0] == "gy" else 1)
            free[link] = max(free.get(link, 0.0), at) + cost
            ready.append((free[link] + 1.5, phase + 1, k))
    return out


def kernel(sizes, pieces, rows, width, *refs):
    bits, core, orders = plan(sizes)
    nb = len(bits)
    rest = [i for i in range(nb) if i != core]
    p_ref, grad_ref, total_ref, own = refs[:4]
    recv = refs[4 : 4 + nb]
    mine, got, own_sem, send_sem, recv_sem, tot_send, tot_recv = refs[4 + nb :]
    here = {a: lax.axis_index(a) for a in AXES}
    at = [lax.rem(here[a] // w, 2) for a, w in bits]

    def partner(i):
        a, w = bits[i]
        return {a: here[a] + w - 2 * w * at[i]}

    peers = [
        [{a: lax.rem(here[a] + k, n)} for k in range(1, n)] for a, n in zip(AXES, sizes)
    ]
    barrier = pltpu.get_barrier_semaphore()
    for row in peers:
        for peer in row:
            pl.semaphore_signal(barrier, inc=1, device_id=peer, device_id_type=MESH)
    pl.semaphore_wait(barrier, sum(len(row) for row in peers))

    step = width // len(pieces)

    def source(k, which):
        index = tuple(which if i == core else slice(None) for i in range(nb))
        return p_ref.at[index + (slice(None), pl.ds(k * step, step))]

    def local(k):
        return pltpu.make_async_copy(source(k, at[core]), own.at[k], own_sem.at[k])

    def view(k, chosen):
        return own.at[(k,) + tuple(chosen.get(i, slice(None)) for i in rest)]

    def remote(phase, k):
        if phase == 0:
            src, i = source(k, 1 - at[core]), core
        else:
            order = orders[pieces[k]]
            i = order[phase - 1]
            chosen = {j: at[j] for j in order[: phase - 1]}
            chosen[i] = 1 - at[i]
            src = view(k, chosen)
        return pltpu.make_async_remote_copy(
            src_ref=src,
            dst_ref=recv[phase].at[k],
            send_sem=send_sem.at[phase, k],
            recv_sem=recv_sem.at[phase, k],
            device_id=partner(i),
            device_id_type=MESH,
        )

    def add(phase, k, fixed=None):
        done = orders[pieces[k]][:phase]
        open_bits = [i for i in rest if i not in done]
        loop_bits = [i for i in open_bits if fixed is None or i != fixed[0]]

        def body(n, carry):
            value = {i: lax.rem(n // (1 << j), 2) for j, i in enumerate(loop_bits)}
            if fixed is not None:
                value[fixed[0]] = fixed[1]
            place = (k,) + tuple(value.get(i, at[i]) for i in rest)
            inner = (k,) + tuple(value[i] for i in open_bits)
            own[place] = own[place] + recv[phase][inner]
            return carry

        lax.fori_loop(0, 1 << len(loop_bits), body, 0)

    for k in range(len(pieces)):
        remote(0, k).start()
        local(k).start()
    squares = jnp.zeros((8, 128), jnp.float32)
    for phase, k in events(bits, orders, pieces):
        remote(phase, k).wait_recv()
        if phase == 0:
            local(k).wait()
        if phase < nb - 1:
            i = orders[pieces[k]][phase]
            add(phase, k, (i, 1 - at[i]))
            remote(phase + 1, k).start()
            add(phase, k, (i, at[i]))
        else:
            place = (k,) + tuple(at[i] for i in rest)
            block = own[place] + recv[phase][k]
            grad_ref[:, k * step : (k + 1) * step] = block
            square = block * block
            square = jnp.sum(square.reshape(rows // 8, 8, step), axis=0)
            for c in range(step // 128):
                squares = squares + square[:, c * 128 : (c + 1) * 128]
    slot = 0
    value = jnp.broadcast_to(jnp.sum(squares, keepdims=True), (8, 128))
    for stage, row in enumerate(peers):
        mine[stage] = value
        copies = []
        for peer in row:
            copy = pltpu.make_async_remote_copy(
                src_ref=mine.at[stage],
                dst_ref=got.at[slot],
                send_sem=tot_send.at[slot],
                recv_sem=tot_recv.at[slot],
                device_id=peer,
                device_id_type=MESH,
            )
            copy.start()
            copies.append((copy, slot))
            slot += 1
        for copy, place in copies:
            copy.wait()
            value = value + got[place]
    total_ref[...] = value
    for phase in range(nb):
        for k in range(len(pieces)):
            remote(phase, k).wait_send()


def reduce_gradient(partial, sizes, rows, width):
    bits, core, orders = plan(sizes)
    nb = len(bits)
    pieces = PATTERN
    step = width // len(pieces)
    slots = sum(n - 1 for n in sizes)
    vmem = lambda *shape: pltpu.VMEM(shape, jnp.float32)
    dma = lambda *shape: pltpu.SemaphoreType.DMA(shape)
    return pl.pallas_call(
        functools.partial(kernel, sizes, pieces, rows, width),
        out_shape=(
            jax.ShapeDtypeStruct((rows, width), jnp.float32),
            jax.ShapeDtypeStruct((8, 128), jnp.float32),
        ),
        in_specs=[pl.BlockSpec(memory_space=pl.ANY)],
        out_specs=(pl.BlockSpec(memory_space=pltpu.VMEM),) * 2,
        scratch_shapes=[
            vmem(len(pieces), *[2] * (nb - 1), rows, step),
            *[vmem(len(pieces), *[2] * (nb - 1 - p), rows, step) for p in range(nb)],
            vmem(len(sizes), 8, 128),
            vmem(slots, 8, 128),
            dma(len(pieces)),
            dma(nb, len(pieces)),
            dma(nb, len(pieces)),
            dma(slots),
            dma(slots),
        ],
        compiler_params=pltpu.CompilerParams(
            collective_id=0, has_side_effects=True, vmem_limit_bytes=60 << 20
        ),
    )(partial.reshape([2] * nb + [rows, width]))


def shards(sizes, inputs, cotangent, master, accum):
    rows, width = master.shape
    partial = lax.dot_general(
        inputs, cotangent, (((0,), (0,)), ((), ())), preferred_element_type=jnp.float32
    )
    gradient, total = reduce_gradient(partial, sizes, rows, width)
    squares = total[0, 0]
    limit = 0.5 * jnp.sqrt(jnp.float32(rows * math.prod(sizes) * width))
    factor = limit / jnp.maximum(jnp.sqrt(squares), limit)
    scaled = factor * gradient
    new_accum = accum + scaled * scaled
    new_master = master - 0.5 * scaled / jnp.sqrt(new_accum)
    return (new_master, new_accum)


def solution(mesh):
    sizes = tuple(mesh.shape[a] for a in AXES)
    spec = P(AXES, None)
    return jax.shard_map(
        functools.partial(shards, sizes),
        mesh=mesh,
        in_specs=(spec,) * 4,
        out_specs=(spec, spec),
        check_vma=False,
    )
```

time: 451 us -> 190 us (0.42)
  waiting for transfers between devices: 367 us -> 0 us
  Pallas kernels: 0 us -> 159 us
  blocking collectives: 39.5 us -> 0 us
  between operations: 14.8 us -> 1.39 us
    reduce_scatter x2 -> x0, waiting for transfers between devices: 367 us -> none  [the longest x1 333 us: shards(): lax.psum_scatter(lax.dot_general(inputs, cotangent, (((0,), (0,)), ((), (...]
    pallas_call x0 -> x1, Pallas kernels: none -> 159 us  [reduce_gradient(): pl.pallas_call(functools.partial(kernel, sizes, pieces, rows, width), out...]
    psum x1 -> x0, blocking collectives: 39.5 us -> none  [shards(): squares = lax.psum(jnp.sum(gradient * gradient), ('gx', 'gy', 'gz'))]
  transfers between devices with their start and end apart: 2 -> 0, of which waited for: 2 -> 0; matrix products, arithmetic and copies ran while one was open for 0% -> 0% of each run, Pallas kernels for 0% -> 0%
where the time goes in v1:
time: 190 us; the launch traced here: 189 us
  Pallas kernels  159 us (84%)
  matrix products  25.3 us (13%)
  other arithmetic  2.78 us (1%)
    pallas_call x1, Pallas kernels, reduce_gradient(): pl.pallas_call(functools.partial(kernel, sizes, pieces, rows, width), out...  159 us
    dot_general x1, matrix products, shards(): lax.dot_general(inputs, cotangent, (((0,), (0,)), ((), ())), preferred_el...  25.3 us

profile of v1, /device:TPU:0, one launch (start us, length us, event | category | flops | bytes accessed | tf_op | source)
XLA Modules:
  0.0 189.4 jit_solution(59231775131731383)
XLA Ops:
  0.6 25.3 %fusion = f32[2048,4096]{1,0:T(8,128)} fusion(bf16[1024,2048]{1,0:T(8,128)(2,1)} %param.4, bf16[1024,4096]{1,0:T(8,128)(2,1)} %param.5), kind=kOutput, calls=%fused_computation.2 | convolution fusion | flops 17179869184 | bytes 46137344 | tf_op jit(solution)/shard_map/dot_general | solution.py:203
  26.0 0.0 copy-start
  26.0 0.0 copy-start.1
  26.0 158.7 %shard_map.59 = (f32[64,4096]{1,0:T(8,128)}, f32[8,128]{1,0:T(8,128)}) custom-call(f32[2,2,2,2,2,64,4096]{6,5,4,3,2,1,0:T(8,128)} %bitcast.4), custom_call_target="tpu_custom_call" | custom-call | tf_op jit(solution)/shard_map/pallas_call | solution.py:176
  184.7 1.2 slice.3
  186.6 0.0 copy-done
  186.6 0.0 copy-done.1
  186.6 2.8 %multiply_subtract_fusion = (f32[64,4096]{1,0:T(8,128)}, f32[64,4096]{1,0:T(8,128)}) fusion(f32[64,4096]{1,0:T(8,128)S(1)} %copy-done, f32[64,4096]{1,0:T(8,128)} %get-tuple-element.5, f32[]{:T(128)} %bitcast.1, f32[64,4096]{1,0:T(8,128)S(1)} %copy-done.1), kind=kLoop, calls=%fused_computation | loop fusion | flops 1572864 | bytes 5242884 | tf_op jit(solution)/shard_map/sub | solution.py:212
Async XLA Ops:
  26.0 160.6 %copy-start = (f32[64,4096]{1,0:T(8,128)S(1)}, f32[64,4096]{1,0:T(8,128)}, u32[]{:S(2)}) copy-start(f32[64,4096]{1,0:T(8,128)} %param.6) | copy-start | bytes 3145732
  26.0 160.6 %copy-start.1 = (f32[64,4096]{1,0:T(8,128)S(1)}, f32[64,4096]{1,0:T(8,128)}, u32[]{:S(2)}) copy-start(f32[64,4096]{1,0:T(8,128)} %param.7) | copy-start | bytes 3145732
